TPU v7x, 32 devices: a whole 2x2x4 slice. The times are simulated.
32 devices in a mesh: seq: 8 (over z, x), hid: 4 (over y, core).
Axes of the slice: x: 2, y: 2, z: 4, core: 2. Of those that a mesh axis runs over, the one named last changes fastest.
Arguments:
- hidden: bfloat16 [8192, 4096], P('seq', 'hid'), may hold values from -40 to 40, as said below
- seg_ids: int32 [8192], P('seq'), may hold values from 0 to 31, as said below
- lengths: int32 [32], replicated, may hold values from 64 to 4096, as said below
- owner_slot: int32 [32], replicated, may hold values from 0 to 31, each once
- pool_bias: float32 [4096], P('hid'), may hold values from -3 to 3
Outputs:
- pooled: bfloat16 [32, 4096], P('seq', 'hid')
Inputs may be any that keep to these rules, and one draw needn't show every extreme that they name: `hidden`: float values; each feature's scale differs. `seg_ids`: never falls along the stream; document d occupies exactly lengths[d] consecutive tokens, documents in order. `lengths`: they sum to 8192; one of them is exactly 4096; the first 16 documents each have 1024 // 16 tokens and so fill the first index's tokens; hence at most 16 documents end within one index's tokens, and the first index has exactly 16. `owner_slot`: each row number once.
All inputs are finite; a program needn't handle non-finite values.
Results may differ from a plain program's by a relative error of at most 0.001.
Values may be sent and summed in bfloat16 or wider, within the bound.
A program may use at most 64 MiB of HBM per device.

v0:
```python
import functools

import jax
import jax.numpy as jnp
from jax import lax
from jax.experimental import pallas as pl
from jax.experimental.pallas import tpu as pltpu
from jax.sharding import PartitionSpec as P

MESH = pl.DeviceIdType.MESH
LANES = 128


def kernel(
    n_seq, n_hid, chunks, urgent, pad,
    hidden_hbm, seg_hbm, len_hbm, slot_hbm, bias_hbm,
    out_ref,
    hidden, seg, lens, slots, bias, parts, landed, squares, squares_in,
    load_sems, small_sems, send_sem, recv_sem, sq_send_sem, sq_recv_sem,
):
    me = lax.axis_index("seq")
    my_hid = lax.axis_index("hid")
    tokens, width = hidden.shape
    docs = lens.shape[1]
    per_owner = docs // n_seq
    step = width // chunks
    features = width * n_hid
    peers = [jnp.where(j < me, j, j + 1) for j in range(n_seq - 1)]
    slot_there = [jnp.where(j < me, me - 1, me) for j in range(n_seq - 1)]
    hid_peers = {k: lax.rem(my_hid + k, n_hid) for k in range(1, n_hid)}

    def loader(c):
        cols = pl.ds(c * step, step)
        return pltpu.make_async_copy(hidden_hbm.at[:, cols], hidden.at[:, cols], load_sems.at[c])

    small = [
        pltpu.make_async_copy(src, dst, small_sems.at[i])
        for i, (src, dst) in enumerate(
            ((slot_hbm, slots), (seg_hbm, seg), (len_hbm, lens), (bias_hbm, bias))
        )
    ]
    small[0].start()
    small[1].start()
    loads = [loader(c) for c in range(chunks)]
    pieces = 4
    rows = tokens // pieces
    for c in range(chunks):
        cols = pl.ds(c * step, step)
        for r in range(pieces):
            part = pl.ds(r * rows, rows)
            pltpu.make_async_copy(
                hidden_hbm.at[part, cols], hidden.at[part, cols], load_sems.at[c]
            ).start()
    small[2].start()
    small[3].start()

    barrier = pltpu.get_barrier_semaphore()
    for peer in peers:
        pl.semaphore_signal(barrier, inc=1, device_id={"seq": peer}, device_id_type=MESH)
    for k in range(1, n_hid):
        pl.semaphore_signal(barrier, inc=1, device_id={"hid": hid_peers[k]}, device_id_type=MESH)

    small[0].wait()
    row = lax.broadcasted_iota(jnp.int32, (n_seq * pad, 1), 0)
    inner = row % pad
    row_slot = jnp.where(inner < per_owner, (row // pad) * per_owner + inner, -1)
    doc_iota = lax.broadcasted_iota(jnp.int32, (1, docs), 1).astype(jnp.float32)
    found = jnp.where(row_slot == slots[...], doc_iota + 1.0, 0.0)
    row_doc = jnp.sum(found, axis=1, keepdims=True).astype(jnp.int32) - 1
    small[1].wait()
    picker = jnp.concatenate(
        [
            jnp.where(row_doc == seg[k : k + 1, :], 1.0, 0.0).astype(jnp.bfloat16)
            for k in range(tokens // LANES)
        ],
        axis=1,
    )

    def send(cols, j):
        pltpu.make_async_remote_copy(
            src_ref=parts.at[peers[j], :, cols],
            dst_ref=landed.at[slot_there[j], :, cols],
            send_sem=send_sem,
            recv_sem=recv_sem,
            device_id={"seq": peers[j]},
            device_id_type=MESH,
        ).start()

    for c in range(chunks):
        cols = pl.ds(c * step, step)
        loads[c].wait()
        product = jnp.dot(picker, hidden[:, cols], preferred_element_type=jnp.float32)
        for p in range(n_seq):
            parts[p, :, cols] = product[p * pad : p * pad + per_owner, :]
        if c == 0:
            pl.semaphore_wait(barrier, n_seq - 1 + n_hid - 1)
        for j in range(urgent):
            send(cols, j)
    for j in range(urgent, n_seq - 1):
        send(pl.ds(0, width), j)

    small[2].wait()
    small[3].wait()
    wanted = lax.broadcasted_iota(jnp.int32, (per_owner, 1), 0) + me * per_owner
    my_len = jnp.sum(
        jnp.where(wanted == slots[...], lens[...].astype(jnp.float32), 0.0), axis=1, keepdims=True
    )

    pltpu.make_async_copy(landed, landed, recv_sem).wait()
    total = parts[me]
    for k in range(n_seq - 1):
        total = total + landed[k]
    averages = total / my_len + bias[...]
    lane_sq = jnp.zeros((per_owner, LANES), jnp.float32)
    for j in range(width // LANES):
        piece = averages[:, j * LANES : (j + 1) * LANES]
        lane_sq = lane_sq + piece * piece
    squares[...] = lane_sq

    for k in range(1, n_hid):
        pltpu.make_async_remote_copy(
            src_ref=squares,
            dst_ref=squares_in.at[k - 1],
            send_sem=sq_send_sem,
            recv_sem=sq_recv_sem,
            device_id={"hid": hid_peers[k]},
            device_id_type=MESH,
        ).start()
    pltpu.make_async_copy(landed, landed, send_sem).wait()
    pltpu.make_async_copy(squares_in, squares_in, sq_recv_sem).wait()
    for k in range(n_hid - 1):
        lane_sq = lane_sq + squares_in[k]
    energy = jnp.sum(lane_sq, axis=1, keepdims=True) / features
    out_ref[...] = (averages * lax.rsqrt(energy + 1e-06)).astype(jnp.bfloat16)
    pltpu.make_async_copy(squares_in, squares_in, sq_send_sem).wait()


def local(n_seq, n_hid, hidden, seg_ids, lengths, owner_slot, pool_bias):
    tokens, width = hidden.shape
    docs = lengths.shape[0]
    per_owner = docs // n_seq
    pad = -(-per_owner // 8) * 8
    chunks = 2
    urgent = max(1, n_seq // 4)
    f32 = jnp.float32
    dma = pltpu.SemaphoreType.DMA
    return pl.pallas_call(
        functools.partial(kernel, n_seq, n_hid, chunks, urgent, pad),
        out_shape=pltpu.VMEM((per_owner, width), jnp.bfloat16),
        in_specs=[pl.BlockSpec(memory_space=pl.ANY)] * 5,
        out_specs=pl.BlockSpec(memory_space=pltpu.VMEM),
        scratch_shapes=[
            pltpu.VMEM((tokens, width), jnp.bfloat16),
            pltpu.VMEM((tokens // LANES, LANES), jnp.int32),
            pltpu.VMEM((1, docs), jnp.int32),
            pltpu.VMEM((1, docs), jnp.int32),
            pltpu.VMEM((1, width), f32),
            pltpu.VMEM((n_seq, per_owner, width), f32),
            pltpu.VMEM((n_seq - 1, per_owner, width), f32),
            pltpu.VMEM((per_owner, LANES), f32),
            pltpu.VMEM((n_hid - 1, per_owner, LANES), f32),
            dma((chunks,)),
            dma((4,)),
            dma(()),
            dma(()),
            dma(()),
            dma(()),
        ],
        compiler_params=pltpu.CompilerParams(collective_id=0, has_side_effects=True),
    )(
        hidden,
        seg_ids.reshape(tokens // LANES, LANES),
        lengths.reshape(1, docs),
        owner_slot.reshape(1, docs),
        pool_bias.reshape(1, width),
    )


def solution(mesh):
    placed = (P("seq", "hid"), P("seq"), P(), P(), P("hid"))
    return jax.shard_map(
        functools.partial(local, mesh.shape["seq"], mesh.shape["hid"]),
        mesh=mesh,
        in_specs=placed,
        out_specs=P("seq", "hid"),
        check_vma=False,
    )
```

profile of v0, /device:TPU:0, one launch (start us, length us, event | category | flops | bytes accessed | tf_op | source)
XLA Modules:
  0.0 13.4 jit_solution(2006705680421338349)
XLA Ops:
  0.0 12.8 %shard_map.55 = bf16[4,1024]{1,0:T(4,128)(2,1)S(1)} custom-call(bf16[1024,1024]{1,0:T(8,128)(2,1)} %hidden_hbm.1, s32[8,128]{1,0:T(8,128)} %bitcast.4, s32[1,32]{1,0:T(1,128)} %bitcast.6, s32[1,32]{1,0:T(1,128)} %bitcast.7, f32[1,1024]{1,0:T(1,128)} %bitcast.5), custom_call_target="tpu_custom_call" | custom-call | tf_op jit(solution)/shard_map/pallas_call | solution.py:147
  12.8 0.6 %copy.7 = bf16[4,1024]{1,0:T(4,128)(2,1)} copy(bf16[4,1024]{1,0:T(4,128)(2,1)S(1)} %shard_map.55) | data formatting | bytes 16384
where the time goes:
time: 13.6 us; the launch traced here: 13.4 us
  Pallas kernels  12.8 us (94%)
  local copies, waits for them, and re-layouts  0.6 us (4%)
    pallas_call x1, Pallas kernels, local(): pl.pallas_call(functools.partial(kernel, n_seq, n_hid, chunks, urgent, pa...  12.8 us
    unnamed x1, local copies, waits for them, and re-layouts  0.6 us

commit v1 on v0

v1 whole, which is shorter than its diff:
```python
import functools

import jax
import jax.numpy as jnp
from jax import lax
from jax.experimental import pallas as pl
from jax.experimental.pallas import tpu as pltpu
from jax.sharding import PartitionSpec as P

MESH = pl.DeviceIdType.MESH
LANES = 128
STEPS = 32.0
TOP = 32700.0


def widened(code):
    tiles = code.shape[1] // LANES - 1
    value = code.astype(jnp.int32).astype(jnp.float32)
    unit = jnp.exp2(value[:, tiles * LANES :] * (1.0 / STEPS)) * (1.0 / TOP)
    return [value[:, j * LANES : (j + 1) * LANES] * unit for j in range(tiles)]


def summed(land, group):
    total = widened(land[group, 0])
    for k in range(1, land.shape[1]):
        total = [a + b for a, b in zip(total, widened(land[group, k]))]
    return total


def squared(tiles):
    out = tiles[0] * tiles[0]
    for t in tiles[1:]:
        out = out + t * t
    return out


def kernel(
    n_seq, n_hid, pair, fold, chunks,
    hidden_hbm, seg_hbm, len_hbm, slot_hbm, bias_hbm,
    out_ref,
    hidden, seg, lens, slots, bias, code, land, extra, mine, theirs,
    load_sems, small_sems, send_sems, recv_sems, extra_send, extra_recv, sq_send, sq_recv,
):
    me = lax.axis_index("seq")
    my_hid = lax.axis_index("hid")
    tokens, width = hidden.shape
    docs = lens.shape[1]
    per_owner = docs // n_seq
    block = per_owner * fold
    part = width // fold
    groups = n_hid // pair
    low = lax.rem(my_hid, pair)
    high = my_hid // pair
    features = width * n_hid
    peers = [jnp.where(j < me, j, j + 1) for j in range(n_seq - 1)]

    rows = tokens // chunks
    smalls = [
        pltpu.make_async_copy(src, dst, small_sems.at[i])
        for i, (src, dst) in enumerate(
            ((slot_hbm, slots), (seg_hbm, seg), (len_hbm, lens), (bias_hbm, bias))
        )
    ]
    loads = [
        pltpu.make_async_copy(
            hidden_hbm.at[pl.ds(t * rows, rows), :], hidden.at[pl.ds(t * rows, rows), :], load_sems.at[t]
        )
        for t in range(chunks)
    ]
    for c in smalls:
        c.start()
    for c in loads:
        c.start()

    barrier = pltpu.get_barrier_semaphore()

    def greet(seq, hid):
        pl.semaphore_signal(barrier, inc=1, device_id=(seq, hid), device_id_type=MESH)

    greeted = 0
    for g in range(groups):
        hid = low + pair * lax.rem(high + g, groups)
        for p in peers:
            greet(p, hid)
            greeted += 1
        if g > 0:
            greet(me, hid)
            greeted += 1
    if pair == 2:
        greet(me, my_hid + 1 - 2 * low)
        greeted += 1

        @pl.when((me == 0) & (my_hid == 1))
        def _():
            for p in range(n_seq):
                for g in range(groups):
                    greet(p, pair * g)

    smalls[0].wait()
    row = lax.broadcasted_iota(jnp.int32, (n_seq * block, 1), 0)
    inner = lax.rem(row, block)
    row_slot = (row // block) * per_owner + lax.rem(inner, per_owner)
    row_part = inner // per_owner
    doc = lax.broadcasted_iota(jnp.int32, (1, docs), 1)
    here = row_slot == slots[...]
    row_doc = jnp.sum(jnp.where(here, doc.astype(jnp.float32), 0.0), axis=1, keepdims=True).astype(jnp.int32)
    smalls[1].wait()
    pickers = [
        jnp.concatenate(
            [
                jnp.where(
                    jnp.where(row_part == f, row_doc, -1) == seg[k : k + 1, :], 1.0, 0.0
                ).astype(jnp.bfloat16)
                for k in range(tokens // LANES)
            ],
            axis=1,
        )
        for f in range(fold)
    ]
    smalls[2].wait()
    smalls[3].wait()
    length = lens[...].astype(jnp.float32)
    row_len = jnp.sum(jnp.where(here, length, 0.0), axis=1, keepdims=True)
    row_first = jnp.sum(jnp.where(doc < row_doc, length, 0.0), axis=1, keepdims=True)
    first = (me * tokens).astype(jnp.float32)
    starts = jnp.where((row_first >= first) & (row_first < first + tokens), 1.0, 0.0)
    inverse = 1.0 / row_len
    block_part = lax.broadcasted_iota(jnp.int32, (block, 1), 0) // per_owner
    offset = bias[:, :part]
    for f in range(1, fold):
        offset = jnp.where(block_part == f, bias[:, f * part : (f + 1) * part], offset)

    sums = None
    for t in range(chunks):
        loads[t].wait()
        for f in range(fold):
            term = jnp.dot(
                pickers[f][:, t * rows : (t + 1) * rows],
                hidden[t * rows : (t + 1) * rows, f * part : (f + 1) * part],
                preferred_element_type=jnp.float32,
            )
            sums = term if sums is None else sums + term

    for p in range(n_seq):
        at = slice(p * block, (p + 1) * block)
        share = sums[at] * inverse[at] + starts[at] * offset
        largest = jnp.abs(share[:, :LANES])
        for j in range(1, part // LANES):
            largest = jnp.maximum(largest, jnp.abs(share[:, j * LANES : (j + 1) * LANES]))
        step = jnp.ceil(jnp.log2(jnp.maximum(largest, 1e-30)) * STEPS)
        gain = jnp.exp2(step * (-1.0 / STEPS)) * TOP
        for j in range(part // LANES):
            lanes = slice(j * LANES, (j + 1) * LANES)
            code[p, :, lanes] = jnp.round(share[:, lanes] * gain).astype(jnp.int32).astype(jnp.int16)
        code[p, :, part:] = step.astype(jnp.int32).astype(jnp.int16)

    pl.semaphore_wait(barrier, greeted + jnp.where(low == 0, pair - 1, 0))

    def send(p, hid, g):
        pltpu.make_async_remote_copy(
            src_ref=code.at[p],
            dst_ref=land.at[g, me],
            send_sem=send_sems.at[g],
            recv_sem=recv_sems.at[g],
            device_id=(p, hid),
            device_id_type=MESH,
        ).start()

    for j, p in enumerate(peers):
        for i in range(groups):
            send(p, low + pair * i, lax.rem(high - i + groups, groups))
            if j == 0 and i == 0 and pair == 2:

                @pl.when(low == 0)
                def _():
                    pltpu.make_async_remote_copy(
                        src_ref=code.at[0],
                        dst_ref=extra.at[high, me],
                        send_sem=extra_send,
                        recv_sem=extra_recv,
                        device_id=(0, 1),
                        device_id_type=MESH,
                    ).start()
    for g in range(1, groups):
        send(me, low + pair * lax.rem(high + g, groups), groups - g)
    land[0, me] = code[me]

    most = land.at[0, pl.ds(0, n_seq - 1)]
    pltpu.make_async_copy(most, most, recv_sems.at[0]).wait()
    averages = summed(land, 0)
    lane_sq = squared(averages)
    for g in range(1, groups):
        pltpu.make_async_copy(land.at[g], land.at[g], recv_sems.at[g]).wait()
        lane_sq = lane_sq + squared(summed(land, g))

    if pair == 2:
        ahead = (me == 0) & (my_hid == 0)
        alone = (me == 0) & (my_hid == 1)
        mine[...] = lane_sq

        @pl.when(jnp.logical_not(ahead))
        def _():
            pltpu.make_async_remote_copy(
                src_ref=mine,
                dst_ref=theirs,
                send_sem=sq_send,
                recv_sem=sq_recv,
                device_id=(me, my_hid + 1 - 2 * low),
                device_id_type=MESH,
            ).start()

        @pl.when(alone)
        def _():
            pltpu.make_async_copy(extra, extra, extra_recv).wait()
            rest = squared(summed(extra, 0))
            for g in range(1, groups):
                rest = rest + squared(summed(extra, g))
            theirs[...] = rest

        @pl.when(jnp.logical_not(alone))
        def _():
            pltpu.make_async_copy(theirs, theirs, sq_recv).wait()

        lane_sq = lane_sq + theirs[...]

    energy = jnp.sum(lane_sq, axis=1, keepdims=True)
    total = energy[:per_owner]
    for f in range(1, fold):
        total = total + energy[f * per_owner : (f + 1) * per_owner]
    scale = lax.rsqrt(total / features + 1e-06)
    for f in range(fold):
        for j, tile in enumerate(averages):
            at = f * part + j * LANES
            out_ref[:, at : at + LANES] = (tile[f * per_owner : (f + 1) * per_owner] * scale).astype(jnp.bfloat16)

    pltpu.make_async_copy(most, most, send_sems.at[0]).wait()
    for g in range(1, groups):
        pltpu.make_async_copy(land.at[g], land.at[g], send_sems.at[g]).wait()
    if pair == 2:

        @pl.when(low == 0)
        def _():
            pltpu.make_async_copy(code.at[0], code.at[0], extra_send).wait()

        @pl.when(jnp.logical_not(ahead))
        def _():
            pltpu.make_async_copy(mine, mine, sq_send).wait()


def local(n_seq, n_hid, hidden, seg_ids, lengths, owner_slot, pool_bias):
    tokens, width = hidden.shape
    docs = lengths.shape[0]
    per_owner = docs // n_seq
    fold = max(1, 8 // per_owner)
    pair = 2 if n_hid % 2 == 0 else 1
    groups = n_hid // pair
    block, part = per_owner * fold, width // fold
    chunks = 4
    f32, i32, i16 = jnp.float32, jnp.int32, jnp.int16
    dma = pltpu.SemaphoreType.DMA
    vmem = pltpu.VMEM
    return pl.pallas_call(
        functools.partial(kernel, n_seq, n_hid, pair, fold, chunks),
        out_shape=vmem((per_owner, width), jnp.bfloat16),
        in_specs=[pl.BlockSpec(memory_space=pl.ANY)] * 5,
        out_specs=pl.BlockSpec(memory_space=vmem),
        scratch_shapes=[
            vmem((tokens, width), jnp.bfloat16),
            vmem((tokens // LANES, LANES), i32),
            vmem((1, docs), i32),
            vmem((1, docs), i32),
            vmem((1, width), f32),
            vmem((n_seq, block, part + LANES), i16),
            vmem((groups, n_seq, block, part + LANES), i16),
            vmem((groups, n_seq, block, part + LANES), i16),
            vmem((block, LANES), f32),
            vmem((block, LANES), f32),
            dma((chunks,)),
            dma((4,)),
            dma((groups,)),
            dma((groups,)),
            dma(()),
            dma(()),
            dma(()),
            dma(()),
        ],
        compiler_params=pltpu.CompilerParams(collective_id=0, has_side_effects=True),
    )(
        hidden,
        seg_ids.reshape(tokens // LANES, LANES),
        lengths.reshape(1, docs),
        owner_slot.reshape(1, docs),
        pool_bias.reshape(1, width),
    )


def solution(mesh):
    placed = (P("seq", "hid"), P("seq"), P(), P(), P("hid"))
    return jax.shard_map(
        functools.partial(local, mesh.shape["seq"], mesh.shape["hid"]),
        mesh=mesh,
        in_specs=placed,
        out_specs=P("seq", "hid"),
        check_vma=False,
    )
```

time: 13.6 us -> 12.1 us (0.89)
  Pallas kernels: 12.8 us -> 11.3 us
    pallas_call x1, Pallas kernels: 12.8 us -> 11.3 us  [local(): pl.pallas_call(functools.partial(kernel, n_seq, n_hid, pair, fold, chunks...]
where the time goes in v1:
time: 12.1 us; the launch traced here: 11.9 us
  Pallas kernels  11.3 us (93%)
  local copies, waits for them, and re-layouts  0.6 us (5%)
    pallas_call x1, Pallas kernels, local(): pl.pallas_call(functools.partial(kernel, n_seq, n_hid, pair, fold, chunks...  11.3 us
    unnamed x1, local copies, waits for them, and re-layouts  0.6 us

profile of v1, /device:TPU:0, one launch (start us, length us, event | category | flops | bytes accessed | tf_op | source)
XLA Modules:
  0.0 11.9 jit_solution(17435891823962698294)
XLA Ops:
  0.0 11.3 %shard_map.55 = bf16[4,1024]{1,0:T(4,128)(2,1)S(1)} custom-call(bf16[1024,1024]{1,0:T(8,128)(2,1)} %hidden_hbm.1, s32[8,128]{1,0:T(8,128)} %bitcast.4, s32[1,32]{1,0:T(1,128)} %bitcast.6, s32[1,32]{1,0:T(1,128)} %bitcast.7, f32[1,1024]{1,0:T(1,128)} %bitcast.5), custom_call_target="tpu_custom_call" | custom-call | tf_op jit(solution)/shard_map/pallas_call | solution.py:262
  11.3 0.6 %copy.7 = bf16[4,1024]{1,0:T(4,128)(2,1)} copy(bf16[4,1024]{1,0:T(4,128)(2,1)S(1)} %shard_map.55) | data formatting | bytes 16384

commit v2 on v1

--- a/solution.py
+++ b/solution.py
@@ -9,15 +9,40 @@
 
 MESH = pl.DeviceIdType.MESH
 LANES = 128
-STEPS = 32.0
-TOP = 32700.0
+STEPS = 8.0
+LEAST = 20.0
+STEP_BITS = 8
 
 
 def widened(code):
-    tiles = code.shape[1] // LANES - 1
-    value = code.astype(jnp.int32).astype(jnp.float32)
-    unit = jnp.exp2(value[:, tiles * LANES :] * (1.0 / STEPS)) * (1.0 / TOP)
-    return [value[:, j * LANES : (j + 1) * LANES] * unit for j in range(tiles)]
+    tiles = code.shape[1] // LANES
+    low = -(-STEP_BITS // tiles)
+    top = float((1 << (15 - low)) - 24)
+    words = [code[:, j * LANES : (j + 1) * LANES].astype(jnp.int32) for j in range(tiles)]
+    step = words[0] & ((1 << low) - 1)
+    for j in range(1, tiles):
+        step = step | ((words[j] & ((1 << low) - 1)) << (low * j))
+    unit = jnp.exp2(step.astype(jnp.float32) * (1.0 / STEPS) - LEAST) * (1.0 / top)
+    return [(w >> low).astype(jnp.float32) * unit for w in words]
+
+
+def narrowed(share):
+    tiles = share.shape[1] // LANES
+    low = -(-STEP_BITS // tiles)
+    top = float((1 << (15 - low)) - 24)
+    parts = [share[:, j * LANES : (j + 1) * LANES] for j in range(tiles)]
+    largest = jnp.abs(parts[0])
+    for x in parts[1:]:
+        largest = jnp.maximum(largest, jnp.abs(x))
+    step = jnp.ceil((jnp.log2(jnp.maximum(largest, 2.0**-LEAST)) + LEAST) * STEPS)
+    gain = jnp.exp2(LEAST - step * (1.0 / STEPS)) * top
+    bits = step.astype(jnp.int32)
+    return [
+        (
+            (jnp.round(x * gain).astype(jnp.int32) << low) | ((bits >> (low * j)) & ((1 << low) - 1))
+        ).astype(jnp.int16)
+        for j, x in enumerate(parts)
+    ]
 
 
 def summed(land, group):
@@ -35,10 +60,10 @@
 
 
 def kernel(
-    n_seq, n_hid, pair, fold, chunks,
+    n_seq, n_hid, pair, fold, chunks, direct,
     hidden_hbm, seg_hbm, len_hbm, slot_hbm, bias_hbm,
     out_ref,
-    hidden, seg, lens, slots, bias, code, land, extra, mine, theirs,
+    hidden, seg, lens, slots, bias, code, land, extra, mine, theirs, whole,
     load_sems, small_sems, send_sems, recv_sems, extra_send, extra_recv, sq_send, sq_recv,
 ):
     me = lax.axis_index("seq")
@@ -52,7 +77,6 @@
     low = lax.rem(my_hid, pair)
     high = my_hid // pair
     features = width * n_hid
-    peers = [jnp.where(j < me, j, j + 1) for j in range(n_seq - 1)]
 
     rows = tokens // chunks
     smalls = [
@@ -73,22 +97,25 @@
         c.start()
 
     barrier = pltpu.get_barrier_semaphore()
+    peers = [jnp.where(j < me, j, j + 1) for j in range(n_seq - 1)]
+    same = [low + pair * lax.rem(high + g, groups) for g in range(groups)]
+    near = me < direct
 
     def greet(seq, hid):
         pl.semaphore_signal(barrier, inc=1, device_id=(seq, hid), device_id_type=MESH)
 
-    greeted = 0
-    for g in range(groups):
-        hid = low + pair * lax.rem(high + g, groups)
+    for k in range(1, n_hid):
+        greet(me, lax.rem(my_hid + k, n_hid))
+    for p in peers:
+        greet(p, my_hid)
+
+    @pl.when(near)
+    def _():
         for p in peers:
-            greet(p, hid)
-            greeted += 1
-        if g > 0:
-            greet(me, hid)
-            greeted += 1
+            for hid in same[1:]:
+                greet(p, hid)
+
     if pair == 2:
-        greet(me, my_hid + 1 - 2 * low)
-        greeted += 1
 
         @pl.when((me == 0) & (my_hid == 1))
         def _():
@@ -144,17 +171,15 @@
     for p in range(n_seq):
         at = slice(p * block, (p + 1) * block)
         share = sums[at] * inverse[at] + starts[at] * offset
-        largest = jnp.abs(share[:, :LANES])
-        for j in range(1, part // LANES):
-            largest = jnp.maximum(largest, jnp.abs(share[:, j * LANES : (j + 1) * LANES]))
-        step = jnp.ceil(jnp.log2(jnp.maximum(largest, 1e-30)) * STEPS)
-        gain = jnp.exp2(step * (-1.0 / STEPS)) * TOP
-        for j in range(part // LANES):
-            lanes = slice(j * LANES, (j + 1) * LANES)
-            code[p, :, lanes] = jnp.round(share[:, lanes] * gain).astype(jnp.int32).astype(jnp.int16)
-        code[p, :, part:] = step.astype(jnp.int32).astype(jnp.int16)
-
-    pl.semaphore_wait(barrier, greeted + jnp.where(low == 0, pair - 1, 0))
+        for j, tile in enumerate(narrowed(share)):
+            code[p, :, j * LANES : (j + 1) * LANES] = tile
+
+    pl.semaphore_wait(
+        barrier,
+        n_hid - 1 + n_seq - 1
+        + (direct - jnp.where(near, 1, 0)) * (groups - 1)
+        + jnp.where(low == 0, pair - 1, 0),
+    )
 
     def send(p, hid, g):
         pltpu.make_async_remote_copy(
@@ -166,63 +191,91 @@
             device_id_type=MESH,
         ).start()
 
-    for j, p in enumerate(peers):
-        for i in range(groups):
-            send(p, low + pair * i, lax.rem(high - i + groups, groups))
-            if j == 0 and i == 0 and pair == 2:
-
-                @pl.when(low == 0)
-                def _():
-                    pltpu.make_async_remote_copy(
-                        src_ref=code.at[0],
-                        dst_ref=extra.at[high, me],
-                        send_sem=extra_send,
-                        recv_sem=extra_recv,
-                        device_id=(0, 1),
-                        device_id_type=MESH,
-                    ).start()
-    for g in range(1, groups):
-        send(me, low + pair * lax.rem(high + g, groups), groups - g)
+    def send_extra():
+        pltpu.make_async_remote_copy(
+            src_ref=code.at[0],
+            dst_ref=extra.at[high, me],
+            send_sem=extra_send,
+            recv_sem=extra_recv,
+            device_id=(0, 1),
+            device_id_type=MESH,
+        ).start()
+
+    for p in range(n_seq):
+
+        @pl.when(p != me)
+        def _():
+            if p < direct:
+                for i in range(groups):
+                    send(p, low + pair * i, lax.rem(high - i + groups, groups))
+            else:
+                send(p, my_hid, 0)
+
+        if p < direct:
+
+            @pl.when(p == me)
+            def _():
+                for g in range(1, groups):
+                    send(p, same[g], groups - g)
+
+        if p == 0 and pair == 2:
+            pl.when(low == 0)(send_extra)
     land[0, me] = code[me]
 
     most = land.at[0, pl.ds(0, n_seq - 1)]
     pltpu.make_async_copy(most, most, recv_sems.at[0]).wait()
     averages = summed(land, 0)
     lane_sq = squared(averages)
-    for g in range(1, groups):
-        pltpu.make_async_copy(land.at[g], land.at[g], recv_sems.at[g]).wait()
-        lane_sq = lane_sq + squared(summed(land, g))
-
-    if pair == 2:
-        ahead = (me == 0) & (my_hid == 0)
-        alone = (me == 0) & (my_hid == 1)
+    ahead = (me == 0) & (my_hid == 0)
+    alone = (me == 0) & (my_hid == 1)
+
+    def pass_on(hid, k):
+        return pltpu.make_async_remote_copy(
+            src_ref=mine,
+            dst_ref=theirs.at[k],
+            send_sem=sq_send,
+            recv_sem=sq_recv,
+            device_id=(me, hid),
+            device_id_type=MESH,
+        )
+
+    @pl.when(near)
+    def _():
+        both = lane_sq
+        for g in range(1, groups):
+            pltpu.make_async_copy(land.at[g], land.at[g], recv_sems.at[g]).wait()
+            both = both + squared(summed(land, g))
+        if pair == 2:
+            mine[...] = both
+            pl.when(jnp.logical_not(ahead))(pass_on(my_hid + 1 - 2 * low, 0).start)
+
+            @pl.when(alone)
+            def _():
+                pltpu.make_async_copy(extra, extra, extra_recv).wait()
+                rest = squared(summed(extra, 0))
+                for g in range(1, groups):
+                    rest = rest + squared(summed(extra, g))
+                theirs[0] = rest
+
+            @pl.when(jnp.logical_not(alone))
+            def _():
+                pltpu.make_async_copy(theirs.at[0], theirs.at[0], sq_recv).wait()
+
+            both = both + theirs[0]
+        whole[...] = both
+
+    @pl.when(jnp.logical_not(near))
+    def _():
         mine[...] = lane_sq
-
-        @pl.when(jnp.logical_not(ahead))
-        def _():
-            pltpu.make_async_remote_copy(
-                src_ref=mine,
-                dst_ref=theirs,
-                send_sem=sq_send,
-                recv_sem=sq_recv,
-                device_id=(me, my_hid + 1 - 2 * low),
-                device_id_type=MESH,
-            ).start()
-
-        @pl.when(alone)
-        def _():
-            pltpu.make_async_copy(extra, extra, extra_recv).wait()
-            rest = squared(summed(extra, 0))
-            for g in range(1, groups):
-                rest = rest + squared(summed(extra, g))
-            theirs[...] = rest
-
-        @pl.when(jnp.logical_not(alone))
-        def _():
-            pltpu.make_async_copy(theirs, theirs, sq_recv).wait()
-
-        lane_sq = lane_sq + theirs[...]
-
+        for k in range(1, n_hid):
+            pass_on(lax.rem(my_hid + k, n_hid), k - 1).start()
+        pltpu.make_async_copy(theirs, theirs, sq_recv).wait()
+        both = lane_sq
+        for k in range(n_hid - 1):
+            both = both + theirs[k]
+        whole[...] = both
+
+    lane_sq = whole[...]
     energy = jnp.sum(lane_sq, axis=1, keepdims=True)
     total = energy[:per_owner]
     for f in range(1, fold):
@@ -235,16 +288,21 @@
 
     pltpu.make_async_copy(most, most, send_sems.at[0]).wait()
     for g in range(1, groups):
-        pltpu.make_async_copy(land.at[g], land.at[g], send_sems.at[g]).wait()
+        sent = land.at[g, pl.ds(0, direct)]
+        pltpu.make_async_copy(sent, sent, send_sems.at[g]).wait()
     if pair == 2:
 
         @pl.when(low == 0)
         def _():
             pltpu.make_async_copy(code.at[0], code.at[0], extra_send).wait()
 
-        @pl.when(jnp.logical_not(ahead))
+        @pl.when(near & jnp.logical_not(ahead))
         def _():
             pltpu.make_async_copy(mine, mine, sq_send).wait()
+
+    @pl.when(jnp.logical_not(near))
+    def _():
+        pltpu.make_async_copy(theirs, theirs, sq_send).wait()
 
 
 def local(n_seq, n_hid, hidden, seg_ids, lengths, owner_slot, pool_bias):
@@ -256,11 +314,12 @@
     groups = n_hid // pair
     block, part = per_owner * fold, width // fold
     chunks = 4
+    direct = max(1, n_seq // 2)
     f32, i32, i16 = jnp.float32, jnp.int32, jnp.int16
     dma = pltpu.SemaphoreType.DMA
     vmem = pltpu.VMEM
     return pl.pallas_call(
-        functools.partial(kernel, n_seq, n_hid, pair, fold, chunks),
+        functools.partial(kernel, n_seq, n_hid, pair, fold, chunks, direct),
         out_shape=vmem((per_owner, width), jnp.bfloat16),
         in_specs=[pl.BlockSpec(memory_space=pl.ANY)] * 5,
         out_specs=pl.BlockSpec(memory_space=vmem),
@@ -270,10 +329,11 @@
             vmem((1, docs), i32),
             vmem((1, docs), i32),
             vmem((1, width), f32),
-            vmem((n_seq, block, part + LANES), i16),
-            vmem((groups, n_seq, block, part + LANES), i16),
-            vmem((groups, n_seq, block, part + LANES), i16),
+            vmem((n_seq, block, part), i16),
+            vmem((groups, n_seq, block, part), i16),
+            vmem((groups, n_seq, block, part), i16),
             vmem((block, LANES), f32),
+            vmem((n_hid - 1, block, LANES), f32),
             vmem((block, LANES), f32),
             dma((chunks,)),
             dma((4,)),

time: 12.1 us -> 11.7 us (0.967)
  Pallas kernels: 11.3 us -> 10.9 us
    pallas_call x1, Pallas kernels: 11.3 us -> 10.9 us  [local(): pl.pallas_call(functools.partial(kernel, n_seq, n_hid, pair, fold, chunks...]
where the time goes in v2:
time: 11.7 us; the launch traced here: 11.5 us
  Pallas kernels  10.9 us (93%)
  local copies, waits for them, and re-layouts  0.6 us (5%)
    pallas_call x1, Pallas kernels, local(): pl.pallas_call(functools.partial(kernel, n_seq, n_hid, pair, fold, chunks...  10.9 us
    unnamed x1, local copies, waits for them, and re-layouts  0.6 us

profile of v2, /device:TPU:0, one launch (start us, length us, event | category | flops | bytes accessed | tf_op | source)
XLA Modules:
  0.0 11.5 jit_solution(14055655927463253432)
XLA Ops:
  0.0 10.9 %shard_map.55 = bf16[4,1024]{1,0:T(4,128)(2,1)S(1)} custom-call(bf16[1024,1024]{1,0:T(8,128)(2,1)} %hidden_hbm.1, s32[8,128]{1,0:T(8,128)} %bitcast.4, s32[1,32]{1,0:T(1,128)} %bitcast.6, s32[1,32]{1,0:T(1,128)} %bitcast.7, f32[1,1024]{1,0:T(1,128)} %bitcast.5), custom_call_target="tpu_custom_call" | custom-call | tf_op jit(solution)/shard_map/pallas_call | solution.py:321
  10.9 0.6 %copy.7 = bf16[4,1024]{1,0:T(4,128)(2,1)} copy(bf16[4,1024]{1,0:T(4,128)(2,1)S(1)} %shard_map.55) | data formatting | bytes 16384

commit v3 on v2

--- a/solution.py
+++ b/solution.py
@@ -144,6 +144,16 @@
         )
         for f in range(fold)
     ]
+    sums = None
+    for t in range(2):
+        loads[t].wait()
+        for f in range(fold):
+            term = jnp.dot(
+                pickers[f][:, t * rows : (t + 1) * rows],
+                hidden[t * rows : (t + 1) * rows, f * part : (f + 1) * part],
+                preferred_element_type=jnp.float32,
+            )
+            sums = term if sums is None else sums + term
     smalls[2].wait()
     smalls[3].wait()
     length = lens[...].astype(jnp.float32)
@@ -157,8 +167,7 @@
     for f in range(1, fold):
         offset = jnp.where(block_part == f, bias[:, f * part : (f + 1) * part], offset)
 
-    sums = None
-    for t in range(chunks):
+    for t in range(2, chunks):
         loads[t].wait()
         for f in range(fold):
             term = jnp.dot(
@@ -201,25 +210,28 @@
             device_id_type=MESH,
         ).start()
 
-    for p in range(n_seq):
-
+    def send_near(p):
         @pl.when(p != me)
         def _():
-            if p < direct:
-                for i in range(groups):
-                    send(p, low + pair * i, lax.rem(high - i + groups, groups))
-            else:
-                send(p, my_hid, 0)
-
-        if p < direct:
-
-            @pl.when(p == me)
-            def _():
-                for g in range(1, groups):
-                    send(p, same[g], groups - g)
-
-        if p == 0 and pair == 2:
-            pl.when(low == 0)(send_extra)
+            for i in range(groups):
+                send(p, low + pair * i, lax.rem(high - i + groups, groups))
+
+        @pl.when(p == me)
+        def _():
+            for g in range(1, groups):
+                send(p, same[g], groups - g)
+
+    urgent = (direct + 1) // 2
+    send_near(0)
+    if pair == 2:
+        pl.when(low == 0)(send_extra)
+    for p in range(1, urgent):
+        send_near(p)
+    for p in range(direct, n_seq):
+        pl.when(p != me)(functools.partial(send, p, my_hid, 0))
+    for p in range(urgent, direct):
+        send_near(p)
+
     land[0, me] = code[me]
 
     most = land.at[0, pl.ds(0, n_seq - 1)]

time: 11.7 us -> 11.6 us (level)
  no operation moved by 1% of the time
where the time goes in v3:
time: 11.6 us; the launch traced here: 11.5 us
  Pallas kernels  10.9 us (94%)
  local copies, waits for them, and re-layouts  0.6 us (5%)
    pallas_call x1, Pallas kernels, local(): pl.pallas_call(functools.partial(kernel, n_seq, n_hid, pair, fold, chunks...  10.9 us
    unnamed x1, local copies, waits for them, and re-layouts  0.6 us

profile of v3, /device:TPU:0, one launch (start us, length us, event | category | flops | bytes accessed | tf_op | source)
XLA Modules:
  0.0 11.5 jit_solution(9407250529217810856)
XLA Ops:
  0.0 10.9 %shard_map.55 = bf16[4,1024]{1,0:T(4,128)(2,1)S(1)} custom-call(bf16[1024,1024]{1,0:T(8,128)(2,1)} %hidden_hbm.1, s32[8,128]{1,0:T(8,128)} %bitcast.4, s32[1,32]{1,0:T(1,128)} %bitcast.6, s32[1,32]{1,0:T(1,128)} %bitcast.7, f32[1,1024]{1,0:T(1,128)} %bitcast.5), custom_call_target="tpu_custom_call" | custom-call | tf_op jit(solution)/shard_map/pallas_call | solution.py:333
  10.9 0.6 %copy.7 = bf16[4,1024]{1,0:T(4,128)(2,1)} copy(bf16[4,1024]{1,0:T(4,128)(2,1)S(1)} %shard_map.55) | data formatting | bytes 16384

commit v4 on v3

--- a/solution.py
+++ b/solution.py
@@ -177,19 +177,6 @@
             )
             sums = term if sums is None else sums + term
 
-    for p in range(n_seq):
-        at = slice(p * block, (p + 1) * block)
-        share = sums[at] * inverse[at] + starts[at] * offset
-        for j, tile in enumerate(narrowed(share)):
-            code[p, :, j * LANES : (j + 1) * LANES] = tile
-
-    pl.semaphore_wait(
-        barrier,
-        n_hid - 1 + n_seq - 1
-        + (direct - jnp.where(near, 1, 0)) * (groups - 1)
-        + jnp.where(low == 0, pair - 1, 0),
-    )
-
     def send(p, hid, g):
         pltpu.make_async_remote_copy(
             src_ref=code.at[p],
@@ -221,10 +208,29 @@
             for g in range(1, groups):
                 send(p, same[g], groups - g)
 
+    for p in range(2):
+        at = slice(p * block, (p + 1) * block)
+        share = sums[at] * inverse[at] + starts[at] * offset
+        for j, tile in enumerate(narrowed(share)):
+            code[p, :, j * LANES : (j + 1) * LANES] = tile
+
+    pl.semaphore_wait(
+        barrier,
+        n_hid - 1 + n_seq - 1
+        + (direct - jnp.where(near, 1, 0)) * (groups - 1)
+        + jnp.where(low == 0, pair - 1, 0),
+    )
+
     urgent = (direct + 1) // 2
     send_near(0)
     if pair == 2:
         pl.when(low == 0)(send_extra)
+    for p in range(2, n_seq):
+        at = slice(p * block, (p + 1) * block)
+        share = sums[at] * inverse[at] + starts[at] * offset
+        for j, tile in enumerate(narrowed(share)):
+            code[p, :, j * LANES : (j + 1) * LANES] = tile
+
     for p in range(1, urgent):
         send_near(p)
     for p in range(direct, n_seq):

time: 11.6 us -> 11.6 us (level)
  no operation moved by 1% of the time
where the time goes in v4:
time: 11.6 us; the launch traced here: 11.5 us
  Pallas kernels  10.9 us (94%)
  local copies, waits for them, and re-layouts  0.6 us (5%)
    pallas_call x1, Pallas kernels, local(): pl.pallas_call(functools.partial(kernel, n_seq, n_hid, pair, fold, chunks...  10.9 us
    unnamed x1, local copies, waits for them, and re-layouts  0.6 us

profile of v4, /device:TPU:0, one launch (start us, length us, event | category | flops | bytes accessed | tf_op | source)
XLA Modules:
  0.0 11.5 jit_solution(8631329241410577216)
XLA Ops:
  0.0 10.9 %shard_map.55 = bf16[4,1024]{1,0:T(4,128)(2,1)S(1)} custom-call(bf16[1024,1024]{1,0:T(8,128)(2,1)} %hidden_hbm.1, s32[8,128]{1,0:T(8,128)} %bitcast.4, s32[1,32]{1,0:T(1,128)} %bitcast.6, s32[1,32]{1,0:T(1,128)} %bitcast.7, f32[1,1024]{1,0:T(1,128)} %bitcast.5), custom_call_target="tpu_custom_call" | custom-call | tf_op jit(solution)/shard_map/pallas_call | solution.py:339
  10.9 0.6 %copy.7 = bf16[4,1024]{1,0:T(4,128)(2,1)} copy(bf16[4,1024]{1,0:T(4,128)(2,1)S(1)} %shard_map.55) | data formatting | bytes 16384
